TPU v7x, 32 devices: a whole 2x2x4 slice. The times are simulated.
32 devices in a mesh: leaf: 8 (over z, y), hand: 4 (over x, core).
Axes of the slice: x: 2, y: 2, z: 4, core: 2. Of those that a mesh axis runs over, the one named last changes fastest.
Arguments:
- opp_range: float32 [1024], P('hand'), may hold values from 0.1 to 1
- br_range: float32 [1024], P('hand'), may hold values from 0.001 to 1
- up_weight: bfloat16 [4, 256, 1024], P(None, 'leaf', 'hand'), may hold values from 0.29882812 to 1
- up_parent: int32 [3, 256], replicated, may hold values from 0 to 255
- board_cards: int32 [768, 5], P('leaf'), may hold values from 0 to 51, as said below
- hand_rank: int32 [768, 1024], P('leaf'), may hold values from 0 to 7461
- root_parent: int32 [768], P('leaf'), may hold values from 0 to 255
- br_actions: int32 [768], P('leaf'), may hold values from 1 to 8
- opp_actions: int32 [768, 8], P('leaf'), may hold values from 1 to 8
- leaf_kind: int32 [768, 8, 8], P('leaf'), may hold values from 0 to 1
- leaf_stake: int32 [768, 8, 8], P('leaf'), may hold values from 1 to 400
- opp_weight: bfloat16 [768, 8, 8, 1024], P('leaf', None, None, 'hand'), may hold values from 0.049804688 to 1
Outputs:
- level_values: float32 [4, 256, 1024], P(None, 'leaf', 'hand')
- root_value: float32 [1024], P('hand')
- best_value: float32 [], replicated
Inputs may be any that keep to these rules, and one draw needn't show every extreme that they name: `board_cards`: five different cards for each subtree.
All inputs are finite; a program needn't handle non-finite values.
Results may differ from a plain program's by a relative error of at most 0.0003.
Values may be sent and summed in bfloat16 or wider, within the bound.
A program may use at most 128 MiB of HBM per device.

v0:
```python
import jax
import jax.numpy as jnp
import numpy as np
from jax import lax
from jax.sharding import PartitionSpec as P

PAYOFF_UNIT = 1.0 / 4096.0


def hand_cards(number):
    low_list = []
    high_list = []
    for low_card in range(52):
        for high_card in range(low_card + 1, 52):
            low_list.append(low_card)
            high_list.append(high_card)
    chosen = np.arange(number) * 1326 // number
    return (np.array(low_list, np.int32)[chosen], np.array(high_list, np.int32)[chosen])


def no_shared(low_rows, high_rows, low_cols, high_cols):
    apart_mask = (low_rows[:, None] != low_cols[None, :]) & (
        low_rows[:, None] != high_cols[None, :]
    )
    apart_mask = (
        apart_mask
        & (high_rows[:, None] != low_cols[None, :])
        & (high_rows[:, None] != high_cols[None, :])
    )
    return apart_mask.astype(jnp.float32)


def board_compat(board_cards, low_cols, high_cols):
    hits = (board_cards[:, :, None] == low_cols[None, None, :]) | (
        board_cards[:, :, None] == high_cols[None, None, :]
    )
    return 1.0 - jnp.any(hits, axis=1).astype(jnp.float32)


def local(
    opp_range,
    br_range,
    up_weight,
    up_parent,
    board_cards,
    hand_rank,
    root_parent,
    br_actions,
    opp_actions,
    leaf_kind,
    leaf_stake,
    opp_weight,
):
    levels_count = up_weight.shape[0]
    nodes_dev = up_weight.shape[1]
    hands_dev = opp_range.shape[0]
    boards_dev = board_cards.shape[0]
    actions_max = opp_actions.shape[1]
    hands_all = hand_rank.shape[1]
    node_total = nodes_dev * lax.axis_size("leaf")
    node_start = lax.axis_index("leaf") * nodes_dev
    hand_start = lax.axis_index("hand") * hands_dev
    low_np, high_np = hand_cards(hands_all)
    low_all = jnp.asarray(low_np)
    high_all = jnp.asarray(high_np)
    low_mine = lax.dynamic_slice_in_dim(low_all, hand_start, hands_dev)
    high_mine = lax.dynamic_slice_in_dim(high_all, hand_start, hands_dev)
    compat = board_compat(board_cards, low_mine, high_mine)
    reach_now = opp_range[None, :] * up_weight[0].astype(jnp.float32)
    for level_id in range(1, levels_count + 1):
        gathered = lax.all_gather(reach_now, "leaf", axis=0, tiled=True)
        if level_id < levels_count:
            parents = lax.dynamic_slice_in_dim(up_parent[level_id - 1], node_start, nodes_dev)
            reach_now = jnp.take(gathered, parents, axis=0) * up_weight[level_id].astype(
                jnp.float32
            )
    root_reach = jnp.take(gathered, root_parent, axis=0) * compat
    legal_mask = (jnp.arange(actions_max)[None, None, :] < opp_actions[:, :, None]).astype(
        jnp.float32
    )
    weighted = opp_weight.astype(jnp.float32) * legal_mask[..., None]
    probability = weighted / jnp.sum(weighted, axis=2, keepdims=True)
    leaf_reach = (root_reach[:, None, None, :] * probability).astype(jnp.bfloat16)
    leaf_reach = leaf_reach.reshape(boards_dev, actions_max * actions_max, hands_dev)
    kind_flat = leaf_kind.reshape(boards_dev, -1)
    stake_flat = leaf_stake.reshape(boards_dev, -1).astype(jnp.float32) * PAYOFF_UNIT
    rank_mine = lax.dynamic_slice_in_dim(hand_rank, hand_start, hands_dev, 1)
    zero_block = jnp.zeros(leaf_reach.shape, jnp.float32)
    block_rows = lax.all_gather(leaf_reach, "hand", axis=2, tiled=True)
    count_rows = block_rows.shape[2]
    low_rows = lax.slice_in_dim(low_all, 0, count_rows, axis=0)
    high_rows = lax.slice_in_dim(high_all, 0, count_rows, axis=0)
    apart_mask = no_shared(low_rows, high_rows, low_mine, high_mine).astype(jnp.bfloat16)
    order_sign = (
        jnp.sign(rank_mine[:, None, :] - hand_rank[:, :, None]).astype(jnp.bfloat16)
        * apart_mask[None]
    )
    showdown = zero_block + jnp.einsum(
        "blo,boh->blh", block_rows, order_sign, preferred_element_type=jnp.float32
    )
    folded = zero_block + jnp.einsum(
        "blo,oh->blh", block_rows, apart_mask, preferred_element_type=jnp.float32
    )
    showdown, folded = (showdown, folded)
    payoff = (
        jnp.where(kind_flat[:, :, None] == 1, showdown, folded)
        * stake_flat[:, :, None]
        * compat[:, None, :]
    )
    per_node = jnp.sum(payoff.reshape(boards_dev, actions_max, actions_max, hands_dev), axis=2)
    allowed = jnp.arange(actions_max)[None, :, None] < br_actions[:, None, None]
    sub_value = jnp.max(jnp.where(allowed, per_node, -1e30), axis=1)
    ancestor = root_parent
    contrib_list = [jax.ops.segment_sum(sub_value, ancestor, num_segments=node_total)]
    for level_id in range(levels_count - 1, 0, -1):
        ancestor = jnp.take(up_parent[level_id - 1], ancestor)
        contrib_list.insert(0, jax.ops.segment_sum(sub_value, ancestor, num_segments=node_total))
    level_values = lax.psum_scatter(
        jnp.stack(contrib_list), "leaf", scatter_dimension=1, tiled=True
    )
    local_total = jnp.sum(level_values[0], axis=0)
    root_value = lax.psum(local_total, "leaf") / node_total
    weighted_sum, range_total = lax.psum(
        (jnp.sum(br_range * root_value), jnp.sum(br_range)), "hand"
    )
    best_value = weighted_sum / range_total
    return (level_values, root_value, best_value)


def solution(mesh):
    in_specs = (
        P("hand"),
        P("hand"),
        P(None, "leaf", "hand"),
        P(),
        P("leaf", None),
        P("leaf", None),
        P("leaf"),
        P("leaf"),
        P("leaf", None),
        P("leaf", None, None),
        P("leaf", None, None),
        P("leaf", None, None, "hand"),
    )
    out_specs = (P(None, "leaf", "hand"), P("hand"), P())
    return jax.shard_map(local, mesh=mesh, in_specs=in_specs, out_specs=out_specs, check_vma=False)
```

profile of v0, /device:TPU:13, one launch (start us, length us, event | category | flops | bytes accessed | tf_op | source)
XLA Modules:
  0.0 375.7 jit_solution(3345140147071384075)
XLA Ops:
  7.2 0.8 fusion.27
  8.8 22.0 %all_gather.15 = f32[256,256]{1,0:T(8,128)S(1)} all-gather(f32[32,256]{1,0:T(8,128)S(1)} %convert_multiply_fusion.7), channel_id=1, replica_groups=mesh['leaf'=8,'hand'=4] {'leaf'}, dimensions={0}, use_global_device_ids=true | all-gather | bytes 294912 | tf_op jit(solution)/shard_map/all_gather | solution.py:71
  31.4 0.8 convert_multiply_fusion.6
  32.2 24.5 %all_gather.16 = f32[256,256]{1,0:T(8,128)S(1)} all-gather(f32[32,256]{1,0:T(8,128)S(1)} %convert_multiply_fusion.6), channel_id=1, replica_groups=mesh['leaf'=8,'hand'=4] {'leaf'}, dimensions={0}, use_global_device_ids=true | all-gather | bytes 294912 | tf_op jit(solution)/shard_map/all_gather | solution.py:71
  57.5 0.8 convert_multiply_fusion.5
  58.3 24.4 %all_gather.17 = f32[256,256]{1,0:T(8,128)S(1)} all-gather(f32[32,256]{1,0:T(8,128)S(1)} %convert_multiply_fusion.5), channel_id=1, replica_groups=mesh['leaf'=8,'hand'=4] {'leaf'}, dimensions={0}, use_global_device_ids=true | all-gather | bytes 294912 | tf_op jit(solution)/shard_map/all_gather | solution.py:71
  84.2 24.3 %all_gather.18 = f32[256,256]{1,0:T(8,128)S(1)} all-gather(f32[32,256]{1,0:T(8,128)S(1)} %convert_multiply_fusion.4), channel_id=1, replica_groups=mesh['leaf'=8,'hand'=4] {'leaf'}, dimensions={0}, use_global_device_ids=true | all-gather | bytes 294912 | tf_op jit(solution)/shard_map/all_gather | solution.py:71
  111.3 1.3 gather_fusion.1
  114.2 0.9 or_reduce_fusion
  115.3 7.0 %fusion.9 = bf16[96,64,256]{2,1,0:T(8,128)(2,1)} fusion(f32[96,8,8]{2,1,0:T(8,128)S(1)} %fusion.14, bf16[96,8,8,256]{3,2,1,0:T(8,128)(2,1)} %param.29, f32[96,256]{1,0:T(8,128)S(1)} %get-tuple-element.22), kind=kOutput, calls=%fused_computation.23 | output fusion | flops 11206663 | bytes 6414336 | tf_op jit(solution)/shard_map/div | solution.py:82
  122.6 1.4 gather_fusion.2
  124.1 1.3 gather_fusion.3
  126.2 109.4 %all-gather.2.cloned.1.call-done = bf16[96,64,1024]{2,1,0:T(8,128)(2,1)} async-done(((bf16[96,64,256]{2,1,0:T(8,128)(2,1)}), bf16[96,64,1024]{2,1,0:T(8,128)(2,1)}) %all-gather.2.cloned.1.call-update) | async-done | bytes 12582928 | tf_op jit(solution)/shard_map/all_gather | solution.py:89
  235.7 8.5 %fusion.12 = f32[96,64,256]{2,1,0:T(8,128)S(1)} fusion(bf16[96,64,1024]{2,1,0:T(8,128)(2,1)} %all-gather.2.cloned.1.call-done, s32[256]{0:T(256)S(1)} %dynamic_slice.31, s32[256]{0:T(256)S(1)} %dynamic_slice.30, s32[1024]{0:T(1024)S(1)} %copy-done.4, s32[1024]{0:T(1024)S(1)} %copy-done.3), kind=kOutput, calls=%fused_computation.27 | convolution fusion | flops 3223584768 | bytes 18884608 | tf_op jit(solution)/shard_map/blo,oh->blh/dot_general | solution.py:101
  244.2 28.5 %bitcast_reduce_fusion = f32[96,8,256]{2,1,0:T(8,128)S(1)} fusion(f32[96,64,256]{2,1,0:T(8,128)S(1)} %fusion.12, f32[96,256]{1,0:T(8,128)S(1)} %get-tuple-element.21, f32[96,64]{1,0:T(8,128)S(1)} %copy.27, pred[96,64]{1,0:T(8,128)(4,1)S(1)} %copy.25, bf16[96,64,1024]{2,1,0:T(8,128)(2,1)S(1)} %copy-done.7, s32[96,1024]{1,0:T(8,128)S(1)} %copy-done.2, ...), kind=kOutput, calls=%fused_computation.18 | convolution fusion | flops 3327983616 | bytes 20805632 | tf_op jit(solution)/shard_map/blo,boh->blh/dot_general | solution.py:98
  273.0 1.2 scatter_custom_fusion.1
  274.1 1.2 scatter_custom_fusion.2
  275.3 1.3 scatter_custom_fusion.3
  276.6 1.2 scatter_custom_fusion
  277.8 1.1 pad_maximum_fusion
  278.9 62.2 %reduce-scatter.2.cloned.1.call-done = f32[4,32,256]{2,1,0:T(8,128)} async-done(((f32[4,256,256]{2,1,0:T(8,128)}), f32[4,32,256]{2,1,0:T(8,128)}) %reduce-scatter.2.cloned.1.call-update) | async-done | bytes 131088 | tf_op jit(solution)/shard_map/reduce_scatter | solution.py:118
  341.8 11.6 %psum.21 = f32[256]{0:T(256)S(1)} all-reduce(f32[256]{0:T(256)S(1)} %slice_reduce_fusion), channel_id=1, replica_groups=mesh['leaf'=8,'hand'=4] {'leaf'}, use_global_device_ids=true, to_apply=%region_10.13 | all-reduce | flops 256 | bytes 2048 | tf_op jit(solution)/shard_map/psum | solution.py:122
  353.4 1.2 fusion.26
  354.7 11.8 %all-reduce = (f32[]{:T(128)}, f32[]{:T(128)}) all-reduce(f32[]{:T(128)} %get-tuple-element.6, f32[]{:T(128)} %get-tuple-element.5), channel_id=1, replica_groups=mesh['leaf'=8,'hand'=4] {'hand'}, use_global_device_ids=true, to_apply=%region_12.15 | all-reduce | flops 2 | bytes 16 | tf_op jit(solution)/shard_map/psum | solution.py:123
  (53 shorter events, 10.5 us)
Async XLA Ops:
  7.2 228.5 %all-gather.2.cloned.1.call-start = ((), (), s32[]{:S(2)}) async-start(), calls=%async_computation.1 | async-start | bytes 15728640 | tf_op jit(solution)/shard_map/all_gather | solution.py:89
  115.2 7.1 %copy-start.1 = (s32[96,8,8]{0,2,1:T(8,128)S(1)}, s32[96,8,8]{0,2,1:T(8,128)}, u32[]{:S(2)}) copy-start(s32[96,8,8]{0,2,1:T(8,128)} %param.28) | copy-start | bytes 73732
  115.2 7.2 %copy-start = (s32[96,8,8]{0,2,1:T(8,128)S(1)}, s32[96,8,8]{0,2,1:T(8,128)}, u32[]{:S(2)}) copy-start(s32[96,8,8]{0,2,1:T(8,128)} %param.27) | copy-start | bytes 73732
  115.2 10.1 %copy-start.2 = (s32[96,1024]{1,0:T(8,128)S(1)}, s32[96,1024]{1,0:T(8,128)}, u32[]{:S(2)}) copy-start(s32[96,1024]{1,0:T(8,128)} %param.23) | copy-start | bytes 1179652
  115.2 10.1 %copy-start.6 = (s32[96]{0:T(128)S(1)}, s32[96]{0:T(128)}, u32[]{:S(2)}) copy-start(s32[96]{0:T(128)} %param.25) | copy-start | bytes 1156
  115.3 10.2 %copy-start.3 = (s32[1024]{0:T(1024)S(1)}, s32[1024]{0:T(1024)}, u32[]{:S(2)}) copy-start(s32[1024]{0:T(1024)} %constant.76.clone) | copy-start | bytes 12292
  115.3 10.2 %copy-start.4 = (s32[1024]{0:T(1024)S(1)}, s32[1024]{0:T(1024)}, u32[]{:S(2)}) copy-start(s32[1024]{0:T(1024)} %constant.77.clone) | copy-start | bytes 12292
  122.3 218.8 %reduce-scatter.2.cloned.1.call-start = ((), (), s32[]{:S(2)}) async-start(), calls=%async_computation.2 | async-start | bytes 1179648 | tf_op jit(solution)/shard_map/reduce_scatter | solution.py:118
  235.7 8.5 %copy-start.7 = (bf16[96,64,1024]{2,1,0:T(8,128)(2,1)S(1)}, bf16[96,64,1024]{2,1,0:T(8,128)(2,1)}, u32[]{:S(2)}) copy-start(bf16[96,64,1024]{2,1,0:T(8,128)(2,1)} %all-gather.2.cloned.1.call-done) | copy-start | bytes 37748740
  244.2 109.2 %copy-start.5 = (f32[256]{0:T(256)S(1)}, f32[256]{0:T(256)}, u32[]{:S(2)}) copy-start(f32[256]{0:T(256)} %param.19) | copy-start | bytes 3076
Sparse Core Ops, SparseCore 0:
  122.4 113.2 all-gather.1
  279.0 62.0 reduce-scatter.1
where the time goes:
time: 383 us; the launch traced here: 376 us
  waiting for transfers between devices  172 us (45%)
  blocking collectives  119 us (31%)
  matrix products  37 us (10%)
  other arithmetic  21.8 us (6%)
  between operations  16.7 us (4%)
  local copies, waits for them, and re-layouts  9.85 us (3%)
    all_gather x1, waiting for transfers between devices, local(): block_rows = lax.all_gather(leaf_reach, 'hand', axis=2, tiled=True)  109 us
    all_gather x4, blocking collectives, local(): gathered = lax.all_gather(reach_now, 'leaf', axis=0, tiled=True)  95.2 us
    reduce_scatter x1, waiting for transfers between devices, local(): lax.psum_scatter(jnp.stack(contrib_list), 'leaf', scatter_dimension=1, ti...  62.2 us
    dot_general x1, matrix products, local(): jnp.einsum('blo,boh->blh', block_rows, order_sign, preferred_element_type...  28.5 us
    psum x1, blocking collectives, local(): lax.psum((jnp.sum(br_range * root_value), jnp.sum(br_range)), 'hand')  11.8 us
    psum x1, blocking collectives, local(): root_value = lax.psum(local_total, 'leaf') / node_total  11.6 us
    dot_general x1, matrix products, local(): jnp.einsum('blo,oh->blh', block_rows, apart_mask, preferred_element_type=...  8.49 us
  transfers between devices with their start and end apart: 2, of which 2 were waited for; matrix products, arithmetic and copies ran while one was open for 1% of the time, Pallas kernels for 0%

commit v1 on v0

v1 whole, which is shorter than its diff:
```python
import functools

import jax
import jax.numpy as jnp
import numpy as np
from jax import lax
from jax.experimental import pallas as pl
from jax.experimental.pallas import tpu as pltpu
from jax.sharding import PartitionSpec as P

PAYOFF_UNIT = 1.0 / 4096.0
VMEM_LIMIT = 60 * 1024 * 1024
F32 = jnp.float32
BF16 = jnp.bfloat16


def hand_cards(number):
    low_list = []
    high_list = []
    for low_card in range(52):
        for high_card in range(low_card + 1, 52):
            low_list.append(low_card)
            high_list.append(high_card)
    chosen = np.arange(number) * 1326 // number
    cards = np.zeros((8, number), np.float32)
    cards[0] = np.array(low_list)[chosen]
    cards[1] = np.array(high_list)[chosen]
    return cards


def vmem():
    return pl.BlockSpec(memory_space=pltpu.VMEM)


def hbm():
    return pl.BlockSpec(memory_space=pl.ANY)


def greet(axes_sizes):
    barrier = pltpu.get_barrier_semaphore()
    count = 0
    for axis, size in axes_sizes:
        me = lax.axis_index(axis)
        for dist in range(1, size):
            pl.semaphore_signal(
                barrier,
                inc=1,
                device_id={axis: lax.rem(me + dist, size)},
                device_id_type=pl.DeviceIdType.MESH,
            )
            count += 1
    pl.semaphore_wait(barrier, count)


def push(axis, size, source, target, send_sem, recv_sem):
    me = lax.axis_index(axis)
    copies = []
    for dist in range(1, size):
        peer = lax.rem(me + dist, size)
        copy = pltpu.make_async_remote_copy(
            src_ref=source(peer),
            dst_ref=target,
            send_sem=send_sem.at[dist - 1],
            recv_sem=recv_sem.at[dist - 1],
            device_id={axis: peer},
            device_id_type=pl.DeviceIdType.MESH,
        )
        copy.start()
        copies.append(copy)
    return copies


def sems(size):
    return pltpu.SemaphoreType.DMA((max(size - 1, 1),))


def gather_kernel(leafs, w_ref, a_ref, w_out, a_out, ws, wr, as_, ar, local_sem):
    me = lax.axis_index("leaf")
    greet((("leaf", leafs),))
    own = [
        pltpu.make_async_copy(w_ref, w_out.at[me], local_sem.at[0]),
        pltpu.make_async_copy(a_ref, a_out.at[me], local_sem.at[1]),
    ]
    for copy in own:
        copy.start()
    copies = push("leaf", leafs, lambda peer: w_ref, w_out.at[me], ws, wr)
    copies += push("leaf", leafs, lambda peer: a_ref, a_out.at[me], as_, ar)
    for copy in own + copies:
        copy.wait()


def gather_upper(weights, ancestors, leafs):
    return pl.pallas_call(
        functools.partial(gather_kernel, leafs),
        out_shape=(
            jax.ShapeDtypeStruct((leafs,) + weights.shape, weights.dtype),
            jax.ShapeDtypeStruct((leafs,) + ancestors.shape, ancestors.dtype),
        ),
        in_specs=[vmem(), vmem()],
        out_specs=(vmem(), vmem()),
        scratch_shapes=[sems(leafs), sems(leafs), sems(leafs), sems(leafs), pltpu.SemaphoreType.DMA((2,))],
        compiler_params=pltpu.CompilerParams(
            collective_id=0, has_side_effects=True, vmem_limit_bytes=VMEM_LIMIT
        ),
        name="gather_upper",
    )(weights, ancestors)


def fold_kernel(levels, actions, anc_ref, board_ref, range_ref, cards_ref, upper_ref, stake_ref, weight_ref, out_ref, reach_ref):
    block = stake_ref.shape[0]
    step = pl.program_id(0)

    @pl.when(step == 0)
    def _():
        boards = anc_ref.shape[0]
        leafs, _, nodes_dev, hands = upper_ref.shape
        node_ids = lax.broadcasted_iota(jnp.int32, (boards, leafs * nodes_dev), 1)
        reach = jnp.broadcast_to(range_ref[...], (boards, hands))
        for level in range(levels):
            pick = jnp.where(anc_ref[:, level : level + 1] == node_ids, 1.0, 0.0).astype(BF16)
            table = upper_ref[:, level].reshape(leafs * nodes_dev, hands)
            reach = reach * jnp.dot(pick, table, preferred_element_type=F32)
        low = cards_ref[0:1, :]
        high = cards_ref[1:2, :]
        free = jnp.ones((boards, hands), F32)
        for card in range(5):
            column = board_ref[:, card : card + 1]
            free = jnp.where((column == low) | (column == high), 0.0, free)
        reach_ref[...] = reach * free

    span = actions * actions
    diagonal = lax.broadcasted_iota(jnp.int32, (actions, span), 0) == (
        lax.broadcasted_iota(jnp.int32, (actions, span), 1) // actions
    )
    for i in range(block):
        stake = jnp.broadcast_to(stake_ref[i : i + 1, :], (actions, span))
        stake = jnp.where(diagonal, stake, 0.0)
        legal = jnp.where(stake != 0.0, 1.0, 0.0)
        shown = jnp.maximum(stake, 0.0)
        fold = jnp.maximum(-stake, 0.0)
        shown_hi = jnp.floor(shown * 0.5) * 2.0
        fold_hi = jnp.floor(fold * 0.5) * 2.0
        rows = jnp.concatenate([legal, shown_hi, shown - shown_hi, fold_hi, fold - fold_hi], axis=0)
        sums = jnp.dot(rows.astype(BF16), weight_ref[i], preferred_element_type=F32)
        scale = reach_ref[pl.ds(step * block + i, 1), :] / sums[0:actions]
        part = [sums[k * actions : (k + 1) * actions] for k in range(5)]
        both = jnp.concatenate([(part[1] + part[2]) * scale, (part[3] + part[4]) * scale], axis=0)
        out_ref[2 * actions * i : 2 * actions * (i + 1), :] = both.astype(BF16)


def fold_reach(anc_columns, boards, opp_range, cards_mine, upper, stakes, weights, levels, actions):
    count, span, hands = weights.shape
    block = 8
    whole = lambda array: pl.BlockSpec(array.shape, lambda i: (0,) * array.ndim)
    return pl.pallas_call(
        functools.partial(fold_kernel, levels, actions),
        grid=(count // block,),
        out_shape=jax.ShapeDtypeStruct((count * 2 * actions, hands), BF16),
        in_specs=[
            whole(anc_columns),
            whole(boards),
            whole(opp_range),
            whole(cards_mine),
            whole(upper),
            pl.BlockSpec((block, span), lambda i: (i, 0)),
            pl.BlockSpec((block, span, hands), lambda i: (i, 0, 0)),
        ],
        out_specs=pl.BlockSpec((block * 2 * actions, hands), lambda i: (i, 0)),
        scratch_shapes=[pltpu.VMEM((count, hands), F32)],
        compiler_params=pltpu.CompilerParams(vmem_limit_bytes=VMEM_LIMIT),
        name="fold_reach",
    )(anc_columns, boards, opp_range, cards_mine, upper, stakes, weights)


def swap_kernel(hands, x_ref, out_ref, send, recv, local_sem):
    me = lax.axis_index("hand")
    greet((("hand", hands),))
    own = pltpu.make_async_copy(x_ref.at[me], out_ref.at[me], local_sem)
    own.start()
    for copy in push("hand", hands, lambda peer: x_ref.at[peer], out_ref.at[me], send, recv):
        copy.wait()
    own.wait()


def swap_hands(x, hands):
    return pl.pallas_call(
        functools.partial(swap_kernel, hands),
        out_shape=jax.ShapeDtypeStruct(x.shape, x.dtype),
        in_specs=[vmem()],
        out_specs=vmem(),
        scratch_shapes=[sems(hands), sems(hands), pltpu.SemaphoreType.DMA(())],
        compiler_params=pltpu.CompilerParams(
            collective_id=1, has_side_effects=True, vmem_limit_bytes=VMEM_LIMIT
        ),
        name="swap_hands",
    )(x)


def value_kernel(actions, place_ref, br_ref, rank_ref, board_ref, cards_ref, reach_ref, out_ref, apart_ref):
    parts, rows_all, width = reach_ref.shape
    block, hands = rank_ref.shape
    step = pl.program_id(0)
    low = cards_ref[0:1, :]
    high = cards_ref[1:2, :]

    @pl.when(step == 0)
    def _():
        columns = cards_ref[...].T
        for part in range(parts):
            rows = slice(part * width, (part + 1) * width)
            low_col = columns[rows, 0:1]
            high_col = columns[rows, 1:2]
            hit = (low_col == low) | (low_col == high) | (high_col == low) | (high_col == high)
            apart_ref[rows, :] = jnp.where(hit, 0.0, 1.0).astype(BF16)

    free = jnp.ones((block, hands), F32)
    for card in range(5):
        column = board_ref[:, card : card + 1]
        free = jnp.where((column == low) | (column == high), 0.0, free)

    folded = jnp.zeros((rows_all, hands), F32)
    for part in range(parts):
        folded = folded + jnp.dot(
            reach_ref[part], apart_ref[part * width : (part + 1) * width, :], preferred_element_type=F32
        )
    rank_columns = rank_ref[...].T
    action_ids = lax.broadcasted_iota(jnp.int32, (actions, 1), 0)
    both = 2 * actions
    best_rows = []
    for i in range(block):
        row = rank_ref[i : i + 1, :]
        shown = jnp.zeros((both, hands), F32)
        for part in range(parts):
            rows = slice(part * width, (part + 1) * width)
            apart = apart_ref[rows, :]
            order = (row - rank_columns[rows, i : i + 1]).astype(BF16)
            order = jnp.minimum(jnp.maximum(order, -apart), apart)
            shown = shown + jnp.dot(
                reach_ref[part, i * both : (i + 1) * both, :], order, preferred_element_type=F32
            )
        per_node = shown[0:actions] + folded[i * both + actions : (i + 1) * both]
        allowed = action_ids < br_ref[place_ref[0] + step * block + i]
        best_rows.append(jnp.max(jnp.where(allowed, per_node, -1e30), axis=0, keepdims=True))
    best = jnp.concatenate(best_rows, axis=0) * (free * PAYOFF_UNIT)
    for part in range(parts):
        out_ref[part] = best[:, part * width : (part + 1) * width]


def subtree_values(place, br_actions, ranks, boards, cards, reach, actions):
    parts, rows, width = reach.shape
    hands = ranks.shape[1]
    mine = rows // (2 * actions)
    block = 8
    steps = mine // block
    index = lambda i, place, br: (lax.div(place[0], block) + i, 0)
    return pl.pallas_call(
        functools.partial(value_kernel, actions),
        grid_spec=pltpu.PrefetchScalarGridSpec(
            num_scalar_prefetch=2,
            grid=(steps,),
            in_specs=[
                pl.BlockSpec((block, hands), index),
                pl.BlockSpec((block, boards.shape[1]), index),
                pl.BlockSpec(cards.shape, lambda i, place, br: (0, 0)),
                pl.BlockSpec((parts, block * 2 * actions, width), lambda i, place, br: (0, i, 0)),
            ],
            out_specs=pl.BlockSpec((parts, block, width), lambda i, place, br: (0, i, 0)),
            scratch_shapes=[pltpu.VMEM((hands, hands), BF16)],
        ),
        out_shape=jax.ShapeDtypeStruct((parts, mine, width), F32),
        compiler_params=pltpu.CompilerParams(vmem_limit_bytes=VMEM_LIMIT),
        name="subtree_values",
    )(place, br_actions, ranks, boards, cards, reach)


def level_kernel(
    hands, leafs, levels, nodes_dev, x_ref, anc_ref, br_ref, level_out, root_out, best_out,
    mine, every, tally, send1, recv1, send2, recv2, send3, recv3, local_sem,
):
    hand = lax.axis_index("hand")
    leaf = lax.axis_index("leaf")
    greet((("hand", hands), ("leaf", leafs)))
    own = pltpu.make_async_copy(x_ref.at[hand], mine.at[hand], local_sem)
    own.start()
    for copy in push("hand", hands, lambda peer: x_ref.at[peer], mine.at[hand], send1, recv1):
        copy.wait()
    own.wait()
    copies = push("leaf", leafs, lambda peer: mine, every.at[leaf], send2, recv2)
    own = pltpu.make_async_copy(mine, every.at[leaf], local_sem)
    own.start()
    own.wait()
    for copy in copies:
        copy.wait()
    width = x_ref.shape[2]
    boards = mine.shape[0] * mine.shape[1]
    node_ids = leaf * nodes_dev + lax.broadcasted_iota(jnp.int32, (nodes_dev, boards), 0)

    def add_leaf(source, carry):
        sums, total = carry
        values = every[source].reshape(boards, width)
        coarse = values.astype(BF16)
        fine = (values - coarse.astype(F32)).astype(BF16)
        lines = anc_ref[source]
        pick = jnp.concatenate(
            [jnp.where(lines[k : k + 1, 0:boards] == node_ids, 1.0, 0.0) for k in range(levels)], axis=0
        ).astype(BF16)
        sums = sums + jnp.dot(pick, coarse, preferred_element_type=F32)
        sums = sums + jnp.dot(pick, fine, preferred_element_type=F32)
        return sums, total + jnp.sum(values, axis=0, keepdims=True)

    start = (jnp.zeros((levels * nodes_dev, width), F32), jnp.zeros((1, width), F32))
    sums, total = lax.fori_loop(0, leafs, add_leaf, start)
    for k in range(levels):
        level_out[k] = sums[k * nodes_dev : (k + 1) * nodes_dev]
    root = total / (nodes_dev * leafs)
    root_out[...] = root
    weight = br_ref[...]
    pair = jnp.concatenate(
        [
            jnp.broadcast_to(jnp.sum(weight * root, axis=1, keepdims=True), (8, 128)),
            jnp.broadcast_to(jnp.sum(weight, axis=1, keepdims=True), (8, 128)),
        ],
        axis=0,
    )
    tally[hand] = pair
    copies = push("hand", hands, lambda peer: tally.at[hand], tally.at[hand], send3, recv3)
    for copy in copies:
        copy.wait()
    both = jnp.sum(tally[...], axis=0)
    best_out[...] = both[0:8] / both[8:16]


def level_sums(values, ancestors, br_range, hands, leafs, levels, nodes_dev):
    _, mine, width = values.shape
    return pl.pallas_call(
        functools.partial(level_kernel, hands, leafs, levels, nodes_dev),
        out_shape=(
            jax.ShapeDtypeStruct((levels, nodes_dev, width), F32),
            jax.ShapeDtypeStruct((1, width), F32),
            jax.ShapeDtypeStruct((8, 128), F32),
        ),
        in_specs=[vmem(), vmem(), vmem()],
        out_specs=(vmem(), vmem(), vmem()),
        scratch_shapes=[
            pltpu.VMEM((hands, mine, width), F32),
            pltpu.VMEM((leafs, hands, mine, width), F32),
            pltpu.VMEM((hands, 16, 128), F32),
            sems(hands), sems(hands), sems(leafs), sems(leafs), sems(hands), sems(hands),
            pltpu.SemaphoreType.DMA(()),
        ],
        compiler_params=pltpu.CompilerParams(
            collective_id=2, has_side_effects=True, vmem_limit_bytes=VMEM_LIMIT
        ),
        name="level_sums",
    )(values, ancestors, br_range)


def local(
    opp_range,
    br_range,
    up_weight,
    up_parent,
    board_cards,
    hand_rank,
    root_parent,
    br_actions,
    opp_actions,
    leaf_kind,
    leaf_stake,
    opp_weight,
):
    levels, nodes_dev, hands_dev = up_weight.shape
    boards_dev, hands_all = hand_rank.shape
    actions = opp_actions.shape[1]
    leafs = lax.axis_size("leaf")
    hands = lax.axis_size("hand")
    hand = lax.axis_index("hand")
    mine = boards_dev // hands
    cards = jnp.asarray(hand_cards(hands_all))
    cards_mine = lax.dynamic_slice_in_dim(cards, hand * hands_dev, hands_dev, 1)
    boards = board_cards.astype(F32)

    node_ids = jnp.arange(up_parent.shape[1])
    chain = [root_parent]
    for level in range(levels - 2, -1, -1):
        chosen = jnp.where(chain[0][:, None] == node_ids[None, :], up_parent[level][None, :], 0)
        chain.insert(0, jnp.sum(chosen, axis=1))
    anc_columns = jnp.stack(chain, axis=1)
    lanes = -(-boards_dev // 128) * 128
    anc_rows = jnp.pad(jnp.stack(chain, axis=0), ((0, -levels % 8), (0, lanes - boards_dev)))

    upper, ancestors = gather_upper(up_weight, anc_rows, leafs)

    signed = jnp.where(leaf_kind == 1, leaf_stake, -leaf_stake)
    legal = jnp.arange(actions)[None, None, :] < opp_actions[:, :, None]
    stakes = jnp.where(legal, signed, 0).astype(F32).reshape(boards_dev, actions * actions)
    weights = opp_weight.reshape(boards_dev, actions * actions, hands_dev)
    folded = fold_reach(
        anc_columns, boards, opp_range[None, :], cards_mine, upper, stakes, weights, levels, actions
    )
    reach = swap_hands(folded.reshape(hands, mine * 2 * actions, hands_dev), hands)
    place = jnp.reshape(hand * mine, (1,)).astype(jnp.int32)
    values = subtree_values(place, br_actions, hand_rank.astype(F32), boards, cards, reach, actions)
    level_values, root, best = level_sums(
        values, ancestors, br_range[None, :], hands, leafs, levels, nodes_dev
    )
    return (level_values, root[0], best[0, 0])


def solution(mesh):
    in_specs = (
        P("hand"),
        P("hand"),
        P(None, "leaf", "hand"),
        P(),
        P("leaf", None),
        P("leaf", None),
        P("leaf"),
        P("leaf"),
        P("leaf", None),
        P("leaf", None, None),
        P("leaf", None, None),
        P("leaf", None, None, "hand"),
    )
    out_specs = (P(None, "leaf", "hand"), P("hand"), P())
    return jax.shard_map(local, mesh=mesh, in_specs=in_specs, out_specs=out_specs, check_vma=False)
```

time: 383 us -> 101 us (0.26); the launches traced: 376 us -> 100 us
  waiting for transfers between devices: 172 us -> 0 us
  blocking collectives: 119 us -> 0 us
  Pallas kernels: 0 us -> 86 us
  matrix products: 37 us -> 0 us
  other arithmetic: 21.8 us -> 4.72 us
  between operations: 16.7 us -> 0.69 us
    all_gather x1 -> x0, waiting for transfers between devices: 109 us -> none  [local(): block_rows = lax.all_gather(leaf_reach, 'hand', axis=2, tiled=True)]
    all_gather x4 -> x0, blocking collectives: 95.2 us -> none  [local(): gathered = lax.all_gather(reach_now, 'leaf', axis=0, tiled=True)]
    pallas_call x0 -> x5, Pallas kernels: none -> 86 us  [the longest x1 30.1 us: level_sums(): pl.pallas_call(functools.partial(level_kernel, hands, leafs, levels, node...]
    reduce_scatter x1 -> x0, waiting for transfers between devices: 62.2 us -> none  [local(): lax.psum_scatter(jnp.stack(contrib_list), 'leaf', scatter_dimension=1, ti...]
    dot_general x2 -> x0, matrix products: 37 us -> none  [the longest x1 28.5 us: local(): jnp.einsum('blo,boh->blh', block_rows, order_sign, preferred_element_type...]
    psum x2 -> x0, blocking collectives: 23.4 us -> none  [the longest x1 11.8 us: local(): lax.psum((jnp.sum(br_range * root_value), jnp.sum(br_range)), 'hand')]
    div x1 -> x0, other arithmetic: 6.96 us -> none  [local(): probability = weighted / jnp.sum(weighted, axis=2, keepdims=True)]
    gather x7 -> x0, local copies, waits for them, and re-layouts: 6.49 us -> none  [the longest x3 3.99 us: local(): ancestor = jnp.take(up_parent[level_id - 1], ancestor)]
  transfers between devices with their start and end apart: 2 -> 0, of which waited for: 2 -> 0; matrix products, arithmetic and copies ran while one was open for 1% -> 0% of each run, Pallas kernels for 0% -> 0%
where the time goes in v1:
time: 101 us; the launch traced here: 100 us
  Pallas kernels  86 us (85%)
  local copies, waits for them, and re-layouts  8.88 us (9%)
  other arithmetic  4.72 us (5%)
    pallas_call x1, Pallas kernels, level_sums(): pl.pallas_call(functools.partial(level_kernel, hands, leafs, levels, node...  30.1 us
    pallas_call x1, Pallas kernels, gather_upper(): pl.pallas_call(functools.partial(gather_kernel, leafs), out_shape=(jax.Sh...  18.4 us
    pallas_call x1, Pallas kernels, subtree_values(): pl.pallas_call(functools.partial(value_kernel, actions), grid_spec=pltpu....  14.9 us
    pallas_call x1, Pallas kernels, swap_hands(): pl.pallas_call(functools.partial(swap_kernel, hands), out_shape=jax.Shape...  13.7 us
    pallas_call x1, Pallas kernels, fold_reach(): pl.pallas_call(functools.partial(fold_kernel, levels, actions), grid=(cou...  8.92 us
    unnamed x5, local copies, waits for them, and re-layouts  3.58 us

profile of v1, /device:TPU:13, one launch (start us, length us, event | category | flops | bytes accessed | tf_op | source)
XLA Modules:
  0.0 100.3 jit_solution(2032292486073535205)
XLA Ops:
  0.6 0.8 fusion.3
  1.4 0.8 select_reduce_fusion.2
  2.3 0.2 select_reduce_fusion.1
  2.5 0.2 select_reduce_fusion
  2.6 0.7 pad_add_fusion.1
  3.3 0.6 pad.4.a_ref
  3.9 18.4 %gather_upper.1 = (bf16[8,4,32,256]{3,2,1,0:T(8,128)(2,1)}, s32[8,8,128]{2,1,0:T(8,128)}) custom-call(bf16[4,32,256]{2,1,0:T(8,128)(2,1)} %w_ref.1, s32[8,128]{1,0:T(8,128)} %pad.4.a_ref), custom_call_target="tpu_custom_call" | custom-call | tf_op jit(solution)/shard_map/gather_upper/pallas_call | solution.py:93
  22.4 0.7 pad_add_fusion
  23.0 0.7 copy.32.anc_ref
  23.8 1.3 %constant_dynamic-slice_fusion.cards_ref = f32[8,256]{1,0:T(8,128)} fusion(f32[8,1024]{1,0:T(8,128)} %constant.16.clone.cards_ref, s32[]{:T(128)S(6)} %select_n.24), kind=kLoop, calls=%fused_computation.13 | loop fusion | bytes 16388 | tf_op jit(solution)/shard_map/dynamic_slice | solution.py:380
  25.0 0.8 copy.31
  25.8 0.6 convert_element_type.10.board_ref
  26.4 0.8 fusion.2
  27.2 0.0 copy-start
  27.2 0.7 copy.33.stake_ref
  27.9 8.9 %fold_reach.1 = bf16[1536,256]{1,0:T(8,128)(2,1)} custom-call(s32[96,4]{1,0:T(8,128)} %copy.32.anc_ref, f32[96,5]{1,0:T(8,128)} %convert_element_type.10.board_ref, f32[1,256]{1,0:T(1,128)} %bitcast.33, f32[8,256]{1,0:T(8,128)} %constant_dynamic-slice_fusion.cards_ref, bf16[8,4,32,256]{3,2,1,0:T(8,128)(2,1)} %get-tuple-element.8.upper_ref, ...), custom_call_target="tpu_custom_call" | custom-call | tf_op jit(solution)/shard_map/fold_reach/pallas_call | solution.py:155
  36.9 13.7 %swap_hands.1.reach_ref = bf16[4,384,256]{2,1,0:T(8,128)(2,1)} custom-call(bf16[4,384,256]{2,1,0:T(8,128)(2,1)} %bitcast.20), custom_call_target="tpu_custom_call" | custom-call | tf_op jit(solution)/shard_map/swap_hands/pallas_call | solution.py:186
  50.6 0.0 copy-done
  50.6 0.8 convert_element_type.9.rank_ref
  51.3 14.9 %subtree_values.1.x_ref = f32[4,24,256]{2,1,0:T(8,128)} custom-call(s32[1]{0:T(128)} %bitcast.place_ref, s32[96]{0:T(128)} %br_ref.1, f32[96,1024]{1,0:T(8,128)} %convert_element_type.9.rank_ref, f32[96,5]{1,0:T(8,128)} %convert_element_type.10.board_ref, f32[8,1024]{1,0:T(8,128)} %constant.16.clone.cards_ref, bf16[4,384,256]{2,1,0:T(8,128)(2,1)} %swap_hands.1.reach_ref), custom_call_target="tpu_custom_call" | custom-call | tf_op jit(solution)/shard_map/subtree_values/pallas_call | solution.py:256
  66.2 30.1 %level_sums.1 = (f32[4,32,256]{2,1,0:T(8,128)}, f32[1,256]{1,0:T(1,128)}, f32[8,128]{1,0:T(8,128)}) custom-call(f32[4,24,256]{2,1,0:T(8,128)} %subtree_values.1.x_ref, s32[8,8,128]{2,1,0:T(8,128)} %get-tuple-element.9.anc_ref, f32[1,256]{1,0:T(1,128)} %bitcast.34), custom_call_target="tpu_custom_call" | custom-call | tf_op jit(solution)/shard_map/level_sums/pallas_call | solution.py:335
  96.3 1.2 %slice.15 = f32[1,1]{1,0:T(1,128)} slice(f32[8,128]{1,0:T(8,128)} %get-tuple-element.12), slice={[0:1], [0:1]} | slice | bytes 8 | tf_op jit(solution)/shard_map/slice | solution.py:407
  97.5 1.6 %copy.36 = f32[4,32,256]{2,1,0:T(8,128)} copy(f32[4,32,256]{2,1,0:T(8,128)} %get-tuple-element.19) | data formatting | bytes 262144
  99.1 1.2 %copy.37 = f32[256]{0:T(256)} copy(f32[256]{0:T(256)} %bitcast.35) | data formatting | bytes 2048
Async XLA Ops:
  27.2 23.3 %copy-start = (s32[96,1024]{1,0:T(8,128)S(1)}, s32[96,1024]{1,0:T(8,128)}, u32[]{:S(2)}) copy-start(s32[96,1024]{1,0:T(8,128)} %param.18) | copy-start | bytes 1179652

commit v2 on v0

v2 whole, which is shorter than its diff:
```python
import functools

import jax
import jax.numpy as jnp
import numpy as np
from jax import lax
from jax.experimental import pallas as pl
from jax.experimental.pallas import tpu as pltpu
from jax.sharding import PartitionSpec as P

PAYOFF_UNIT = 1.0 / 4096.0
VMEM_LIMIT = 60 * 1024 * 1024
F32 = jnp.float32
BF16 = jnp.bfloat16


def hand_cards(number):
    low_list = []
    high_list = []
    for low_card in range(52):
        for high_card in range(low_card + 1, 52):
            low_list.append(low_card)
            high_list.append(high_card)
    chosen = np.arange(number) * 1326 // number
    cards = np.zeros((8, number), np.float32)
    cards[0] = np.array(low_list)[chosen]
    cards[1] = np.array(high_list)[chosen]
    cards[2] = np.exp2(np.arange(number) * 0.6180339887498949 % 1.0)
    cards[3] = 1.0 / cards[2]
    return cards


def vmem():
    return pl.BlockSpec(memory_space=pltpu.VMEM)


def hbm():
    return pl.BlockSpec(memory_space=pl.ANY)


def greet(axes_sizes):
    barrier = pltpu.get_barrier_semaphore()
    count = 0
    for axis, size in axes_sizes:
        me = lax.axis_index(axis)
        for dist in range(1, size):
            pl.semaphore_signal(
                barrier,
                inc=1,
                device_id={axis: lax.rem(me + dist, size)},
                device_id_type=pl.DeviceIdType.MESH,
            )
            count += 1
    pl.semaphore_wait(barrier, count)


def push(axis, size, source, target, sem):
    me = lax.axis_index(axis)
    copies = []
    for dist in range(1, size):
        peer = lax.rem(me + dist, size)
        copies.append(push_one(axis, peer, source(peer), target, sem, dist))
    return copies


def push_one(axis, peer, source, target, sem, dist):
    send_sem, recv_sem = sem
    copy = pltpu.make_async_remote_copy(
        src_ref=source,
        dst_ref=target,
        send_sem=send_sem.at[dist - 1],
        recv_sem=recv_sem.at[dist - 1],
        device_id={axis: peer},
        device_id_type=pl.DeviceIdType.MESH,
    )
    copy.start()
    return copy


def sems(*shape):
    return pltpu.SemaphoreType.DMA(shape[:-1] + (max(shape[-1] - 1, 1),))


def columns_of(ref, pad_ref):
    lines, count = ref.shape
    pad_ref[...] = jnp.zeros(pad_ref.shape, F32)
    pad_ref[0:lines, 0:count] = ref[...].astype(F32)
    return pad_ref[...].T


def opponent_kernel(
    leafs, hands, levels, actions,
    upper_ref, parent_ref, root_ref, board_ref, range_ref, cards_ref, opp_ref, kind_ref, stake_ref, weight_ref,
    ratio_out, reach_out, anc_out,
    every, weights, ratio, reach, anc, pad, stake_lines, stake_rows,
    up_s, up_r, anc_s, anc_r, ratio_s, ratio_r, reach_s, reach_r, load_sem, own_sem,
):
    leaf = lax.axis_index("leaf")
    hand = lax.axis_index("hand")
    mine = weights.shape[1]
    width = weights.shape[3]
    boards = hands * mine
    span = actions * actions
    both = 2 * actions
    nodes_dev = upper_ref.shape[1]
    nodes = leafs * nodes_dev

    loads = []
    for dist in range(hands):
        part = lax.rem(hand + dist + 1, hands)
        load = pltpu.make_async_copy(
            weight_ref.at[pl.ds(part * mine, mine)], weights.at[part], load_sem.at[dist]
        )
        load.start()
        loads.append(load)
    own_upper = pltpu.make_async_copy(upper_ref, every.at[leaf], own_sem.at[0])
    own_upper.start()
    greet((("leaf", leafs), ("hand", hands)))
    up_copies = push("leaf", leafs, lambda peer: upper_ref, every.at[leaf], (up_s, up_r))

    stake_lines[...] = jnp.zeros(stake_lines.shape, F32)
    reply_ids = lax.broadcasted_iota(jnp.int32, (actions, boards), 0)
    for a in range(actions):
        lines = slice(a * actions, (a + 1) * actions)
        stake = stake_ref[lines, :]
        signed = jnp.where(kind_ref[lines, :] == 1, stake, -stake)
        legal = reply_ids < opp_ref[a : a + 1, :]
        stake_lines[lines, 0:boards] = jnp.where(legal, signed, 0).astype(F32)
    stake_rows[...] = stake_lines[...].T

    node_column = lax.broadcasted_iota(jnp.int32, (nodes, boards), 0)
    anc[...] = jnp.zeros(anc.shape, F32)
    line = root_ref[...]
    anc[levels - 1 : levels, 0:boards] = line.astype(F32)
    for level in range(levels - 2, -1, -1):
        parents = jnp.broadcast_to(parent_ref[level : level + 1, :], (8, nodes)).astype(F32)
        column = parents.T[:, 0:1]
        line_f = jnp.sum(jnp.where(node_column == line, column, 0.0), axis=0, keepdims=True)
        anc[level : level + 1, 0:boards] = line_f
        line = line_f.astype(jnp.int32)
    anc_columns = anc[...].T.astype(jnp.int32)

    diagonal = lax.broadcasted_iota(jnp.int32, (actions, span), 0) == (
        lax.broadcasted_iota(jnp.int32, (actions, span), 1) // actions
    )

    own_lanes = pl.ds(pl.multiple_of(hand * width, width), width)
    spread = cards_ref[2:3, own_lanes]

    def fold_part(part, target):
        def eight(k, carry):
            lines = stake_rows[pl.ds(pl.multiple_of(part * mine + k * 8, 8), 8), :]
            for i in range(8):
                stake = jnp.broadcast_to(lines[i : i + 1, :], (actions, span))
                stake = jnp.where(diagonal, stake, 0.0)
                legal = jnp.where(stake != 0.0, 1.0, 0.0)
                shown = jnp.maximum(stake, 0.0)
                fold = jnp.maximum(-stake, 0.0)
                shown_hi = jnp.floor(shown * 0.5) * 2.0
                fold_hi = jnp.floor(fold * 0.5) * 2.0
                rows = jnp.concatenate([legal, shown_hi, shown - shown_hi, fold_hi, fold - fold_hi], axis=0)
                sums = jnp.dot(rows.astype(BF16), weights[part, k * 8 + i], preferred_element_type=F32)
                piece = [sums[j * actions : (j + 1) * actions] for j in range(5)]
                scale = spread / piece[0]
                pair = jnp.concatenate(
                    [(piece[1] + piece[2]) * scale, (piece[3] + piece[4]) * scale], axis=0
                )
                place = pl.multiple_of((k * 8 + i) * both, both)
                target[part, pl.ds(place, both), :] = pair.astype(BF16)
            return carry

        lax.fori_loop(0, mine // 8, eight, 0)

    ratio_copies = []
    for dist in range(1, hands):
        part = lax.rem(hand + dist, hands)
        loads[dist - 1].wait()
        fold_part(part, ratio)
        ratio_copies.append(
            push_one("hand", part, ratio.at[part], ratio_out.at[hand], (ratio_s, ratio_r), dist)
        )
    anc_copies = push("leaf", leafs, lambda peer: anc, anc_out.at[leaf], (anc_s, anc_r))
    anc_out[leaf] = anc[...]

    low = cards_ref[0:1, own_lanes]
    high = cards_ref[1:2, own_lanes]
    board_columns = columns_of(board_ref, pad)
    free = jnp.ones((boards, width), F32)
    for card in range(5):
        column = board_columns[0:boards, card : card + 1]
        free = jnp.where((column == low) | (column == high), 0.0, free)

    own_upper.wait()
    for copy in up_copies:
        copy.wait()
    node_ids = lax.broadcasted_iota(jnp.int32, (boards, nodes), 1)
    total = jnp.broadcast_to(range_ref[...], (boards, width))
    for level in range(levels):
        pick = jnp.where(anc_columns[0:boards, level : level + 1] == node_ids, 1.0, 0.0).astype(BF16)
        table = every[:, level].reshape(nodes, width)
        total = total * jnp.dot(pick, table, preferred_element_type=F32)
    total = total * (free * cards_ref[3:4, own_lanes])
    for part in range(hands):
        reach[part] = total[part * mine : (part + 1) * mine]
    reach_copies = push("hand", hands, lambda peer: reach.at[peer], reach_out.at[hand], (reach_s, reach_r))
    reach_out[hand] = reach[hand]

    loads[hands - 1].wait()
    fold_part(hand, ratio)
    ratio_out[hand] = ratio[hand]
    for copy in anc_copies + ratio_copies + reach_copies:
        copy.wait()


def opponent(upper, parents, roots, boards, opp_range, cards, opp_actions, kinds, stakes, weights, leafs, hands, actions):
    levels, nodes_dev, width = upper.shape
    count, span, _ = weights.shape
    mine = count // hands
    lanes = -(-count // 128) * 128
    return pl.pallas_call(
        functools.partial(opponent_kernel, leafs, hands, levels, actions),
        out_shape=(
            jax.ShapeDtypeStruct((hands, mine * 2 * actions, width), BF16),
            jax.ShapeDtypeStruct((hands, mine, width), F32),
            jax.ShapeDtypeStruct((leafs, 8, lanes), F32),
        ),
        in_specs=[vmem()] * 9 + [hbm()],
        out_specs=(vmem(), vmem(), vmem()),
        scratch_shapes=[
            pltpu.VMEM((leafs, levels, nodes_dev, width), BF16),
            pltpu.VMEM((hands, mine, span, width), BF16),
            pltpu.VMEM((hands, mine * 2 * actions, width), BF16),
            pltpu.VMEM((hands, mine, width), F32),
            pltpu.VMEM((8, lanes), F32),
            pltpu.VMEM((8, lanes), F32),
            pltpu.VMEM((span, lanes), F32),
            pltpu.VMEM((lanes, span), F32),
            sems(leafs), sems(leafs), sems(leafs), sems(leafs),
            sems(hands), sems(hands), sems(hands), sems(hands),
            pltpu.SemaphoreType.DMA((hands,)),
            pltpu.SemaphoreType.DMA((1,)),
        ],
        compiler_params=pltpu.CompilerParams(
            collective_id=0, has_side_effects=True, vmem_limit_bytes=VMEM_LIMIT
        ),
        name="opponent",
    )(upper, parents, roots, boards, opp_range, cards, opp_actions, kinds, stakes, weights)


def responder_kernel(
    hands, leafs, levels, nodes_dev, actions,
    ratio_ref, reach_ref, anc_ref, actions_ref, rank_ref, board_ref, cards_ref, range_ref,
    level_out, root_out, best_out,
    apart_ref, pad, board_columns, ready, mine, every, tally,
    hand_s, hand_r, leaf_s, leaf_r, best_s, best_r, own_sem,
):
    hand = lax.axis_index("hand")
    leaf = lax.axis_index("leaf")
    _, count, width = mine.shape
    all_hands = rank_ref.shape[1]
    both = 2 * actions
    chunks = count // 8
    low = cards_ref[0:1, :]
    high = cards_ref[1:2, :]
    columns = cards_ref[...].T
    for part in range(hands):
        rows = slice(part * width, (part + 1) * width)
        low_col = columns[rows, 0:1]
        high_col = columns[rows, 1:2]
        hit = (low_col == low) | (low_col == high) | (high_col == low) | (high_col == high)
        apart_ref[rows, :] = jnp.where(hit, 0.0, 1.0).astype(BF16)
    board_columns[...] = columns_of(board_ref, pad)
    greet((("hand", hands), ("leaf", leafs)))
    action_ids = lax.broadcasted_iota(jnp.int32, (actions, 1), 0)

    def values(chunk):
        first = pl.multiple_of(hand * count + chunk * 8, 8)
        cards_on = board_columns[pl.ds(first, 8), :]
        free = jnp.ones((8, all_hands), F32)
        for card in range(5):
            column = cards_on[:, card : card + 1]
            free = jnp.where((column == low) | (column == high), 0.0, free)
        ranks = rank_ref[pl.ds(first, 8), :].astype(F32)
        rank_columns = ranks.T
        lines = []
        folded = jnp.zeros((8 * both, all_hands), F32)
        for part in range(hands):
            pieces = []
            for i in range(8):
                b = chunk * 8 + i
                row = ratio_ref[part, b * both : (b + 1) * both, :].astype(F32)
                pieces.append((row * reach_ref[part, b : b + 1, :]).astype(BF16))
            lines.append(pieces)
            folded = folded + jnp.dot(
                jnp.concatenate(pieces, axis=0),
                apart_ref[part * width : (part + 1) * width, :],
                preferred_element_type=F32,
            )
        best_rows = []
        for i in range(8):
            shown = jnp.zeros((both, all_hands), F32)
            for part in range(hands):
                rows = slice(part * width, (part + 1) * width)
                apart = apart_ref[rows, :]
                order = (ranks[i : i + 1, :] - rank_columns[rows, i : i + 1]).astype(BF16)
                order = jnp.minimum(jnp.maximum(order, -apart), apart)
                shown = shown + jnp.dot(lines[part][i], order, preferred_element_type=F32)
            per_node = shown[0:actions] + folded[i * both + actions : (i + 1) * both]
            allowed = action_ids < actions_ref[first + i]
            best_rows.append(jnp.max(jnp.where(allowed, per_node, -1e30), axis=0, keepdims=True))
        best = jnp.concatenate(best_rows, axis=0) * (free * PAYOFF_UNIT)
        for part in range(hands):
            ready[part, chunk * 8 : (chunk + 1) * 8, :] = best[:, part * width : (part + 1) * width]

    def to_hands(chunk):
        rows = pl.ds(chunk * 8, 8)
        copies = push(
            "hand", hands, lambda peer: ready.at[peer, rows], mine.at[hand, rows],
            (hand_s.at[chunk], hand_r.at[chunk]),
        )
        mine[hand, chunk * 8 : (chunk + 1) * 8, :] = ready[hand, chunk * 8 : (chunk + 1) * 8, :]
        return copies

    def to_leafs(chunk, copies):
        for copy in copies:
            copy.wait()
        rows = pl.ds(chunk * 8, 8)
        return push(
            "leaf", leafs, lambda peer: mine.at[:, rows], every.at[leaf, :, rows],
            (leaf_s.at[chunk], leaf_r.at[chunk]),
        )

    leaf_copies = []
    hand_copies = None
    for chunk in range(chunks):
        values(chunk)
        sent = to_hands(chunk)
        if chunk > 0:
            leaf_copies += to_leafs(chunk - 1, hand_copies)
        hand_copies = sent
    leaf_copies += to_leafs(chunks - 1, hand_copies)
    every[leaf] = mine[...]

    boards = hands * count
    node_ids = leaf * nodes_dev + lax.broadcasted_iota(jnp.int32, (nodes_dev, boards), 0)
    node_ids = node_ids.astype(F32)
    for copy in leaf_copies:
        copy.wait()

    def add_leaf(source, carry):
        sums, total = carry
        block = every[source].reshape(boards, width)
        coarse = block.astype(BF16)
        fine = (block - coarse.astype(F32)).astype(BF16)
        lines = anc_ref[source]
        pick = jnp.concatenate(
            [jnp.where(lines[k : k + 1, 0:boards] == node_ids, 1.0, 0.0) for k in range(levels)], axis=0
        ).astype(BF16)
        sums = sums + jnp.dot(pick, coarse, preferred_element_type=F32)
        sums = sums + jnp.dot(pick, fine, preferred_element_type=F32)
        return sums, total + jnp.sum(block, axis=0, keepdims=True)

    start = (jnp.zeros((levels * nodes_dev, width), F32), jnp.zeros((1, width), F32))
    sums, total = lax.fori_loop(0, leafs, add_leaf, start)
    root = total / (nodes_dev * leafs)
    root_out[...] = root
    weight = range_ref[...]
    tally[hand] = jnp.concatenate(
        [
            jnp.broadcast_to(jnp.sum(weight * root, axis=1, keepdims=True), (8, 128)),
            jnp.broadcast_to(jnp.sum(weight, axis=1, keepdims=True), (8, 128)),
        ],
        axis=0,
    )
    copies = push("hand", hands, lambda peer: tally.at[hand], tally.at[hand], (best_s, best_r))
    for k in range(levels):
        level_out[k] = sums[k * nodes_dev : (k + 1) * nodes_dev]
    for copy in copies:
        copy.wait()
    pair = jnp.sum(tally[...], axis=0)
    best_out[...] = pair[0:1, 0:1] / pair[8:9, 0:1]


def responder(ratio, reach, ancestors, br_actions, ranks, boards, cards, br_range, leafs, hands, nodes_dev, levels, actions):
    _, count, width = reach.shape
    all_hands = ranks.shape[1]
    lanes = ancestors.shape[2]
    chunks = count // 8
    return pl.pallas_call(
        functools.partial(responder_kernel, hands, leafs, levels, nodes_dev, actions),
        out_shape=(
            jax.ShapeDtypeStruct((levels, nodes_dev, width), F32),
            jax.ShapeDtypeStruct((1, width), F32),
            jax.ShapeDtypeStruct((1, 1), F32),
        ),
        in_specs=[vmem()] * 3 + [pl.BlockSpec(memory_space=pltpu.SMEM)] + [vmem()] * 4,
        out_specs=(vmem(), vmem(), vmem()),
        scratch_shapes=[
            pltpu.VMEM((all_hands, all_hands), BF16),
            pltpu.VMEM((8, lanes), F32),
            pltpu.VMEM((lanes, 8), F32),
            pltpu.VMEM((hands, count, width), F32),
            pltpu.VMEM((hands, count, width), F32),
            pltpu.VMEM((leafs, hands, count, width), F32),
            pltpu.VMEM((hands, 16, 128), F32),
            sems(chunks, hands), sems(chunks, hands), sems(chunks, leafs), sems(chunks, leafs),
            sems(hands), sems(hands),
            pltpu.SemaphoreType.DMA(()),
        ],
        compiler_params=pltpu.CompilerParams(
            collective_id=1, has_side_effects=True, vmem_limit_bytes=VMEM_LIMIT
        ),
        name="responder",
    )(ratio, reach, ancestors, br_actions, ranks, boards, cards, br_range)


def local(
    opp_range,
    br_range,
    up_weight,
    up_parent,
    board_cards,
    hand_rank,
    root_parent,
    br_actions,
    opp_actions,
    leaf_kind,
    leaf_stake,
    opp_weight,
):
    levels, nodes_dev, hands_dev = up_weight.shape
    boards_dev, hands_all = hand_rank.shape
    actions = opp_actions.shape[1]
    span = actions * actions
    leafs = lax.axis_size("leaf")
    hands = lax.axis_size("hand")
    cards = jnp.asarray(hand_cards(hands_all))
    boards = board_cards.T
    ratio, reach, ancestors = opponent(
        up_weight,
        up_parent,
        root_parent[None, :],
        boards,
        opp_range[None, :],
        cards,
        opp_actions.T,
        leaf_kind.transpose(1, 2, 0).reshape(span, boards_dev),
        leaf_stake.transpose(1, 2, 0).reshape(span, boards_dev),
        opp_weight.reshape(boards_dev, span, hands_dev),
        leafs,
        hands,
        actions,
    )
    level_values, root, best = responder(
        ratio,
        reach,
        ancestors,
        br_actions,
        hand_rank,
        boards,
        cards,
        br_range[None, :],
        leafs,
        hands,
        nodes_dev,
        levels,
        actions,
    )
    return (level_values, root[0], best[0, 0])


def solution(mesh):
    in_specs = (
        P("hand"),
        P("hand"),
        P(None, "leaf", "hand"),
        P(),
        P("leaf", None),
        P("leaf", None),
        P("leaf"),
        P("leaf"),
        P("leaf", None),
        P("leaf", None, None),
        P("leaf", None, None),
        P("leaf", None, None, "hand"),
    )
    out_specs = (P(None, "leaf", "hand"), P("hand"), P())
    return jax.shard_map(local, mesh=mesh, in_specs=in_specs, out_specs=out_specs, check_vma=False)
```

time: 383 us -> 66.4 us (0.17); the launches traced: 376 us -> 65.2 us
  waiting for transfers between devices: 172 us -> 0 us
  blocking collectives: 119 us -> 0 us
  Pallas kernels: 0 us -> 60 us
  matrix products: 37 us -> 0 us
  other arithmetic: 21.8 us -> 0 us
  between operations: 16.7 us -> 2.41 us
  local copies, waits for them, and re-layouts: 9.85 us -> 2.78 us
    all_gather x1 -> x0, waiting for transfers between devices: 109 us -> none  [local(): block_rows = lax.all_gather(leaf_reach, 'hand', axis=2, tiled=True)]
    all_gather x4 -> x0, blocking collectives: 95.2 us -> none  [local(): gathered = lax.all_gather(reach_now, 'leaf', axis=0, tiled=True)]
    reduce_scatter x1 -> x0, waiting for transfers between devices: 62.2 us -> none  [local(): lax.psum_scatter(jnp.stack(contrib_list), 'leaf', scatter_dimension=1, ti...]
    pallas_call x0 -> x2, Pallas kernels: none -> 60 us  [the longest x1 37.6 us: responder(): pl.pallas_call(functools.partial(responder_kernel, hands, leafs, levels,...]
    dot_general x2 -> x0, matrix products: 37 us -> none  [the longest x1 28.5 us: local(): jnp.einsum('blo,boh->blh', block_rows, order_sign, preferred_element_type...]
    psum x2 -> x0, blocking collectives: 23.4 us -> none  [the longest x1 11.8 us: local(): lax.psum((jnp.sum(br_range * root_value), jnp.sum(br_range)), 'hand')]
    div x1 -> x0, other arithmetic: 6.96 us -> none  [local(): probability = weighted / jnp.sum(weighted, axis=2, keepdims=True)]
    gather x7 -> x0, local copies, waits for them, and re-layouts: 6.49 us -> none  [the longest x3 3.99 us: local(): ancestor = jnp.take(up_parent[level_id - 1], ancestor)]
  transfers between devices with their start and end apart: 2 -> 0, of which waited for: 2 -> 0; matrix products, arithmetic and copies ran while one was open for 1% -> 0% of each run, Pallas kernels for 0% -> 0%
where the time goes in v2:
time: 66.4 us; the launch traced here: 65.2 us
  Pallas kernels  60 us (90%)
  local copies, waits for them, and re-layouts  2.78 us (4%)
  between operations  2.41 us (4%)
    pallas_call x1, Pallas kernels, responder(): pl.pallas_call(functools.partial(responder_kernel, hands, leafs, levels,...  37.6 us
    pallas_call x1, Pallas kernels, opponent(): pl.pallas_call(functools.partial(opponent_kernel, leafs, hands, levels, a...  22.4 us
    unnamed x2, local copies, waits for them, and re-layouts  2.78 us

profile of v2, /device:TPU:13, one launch (start us, length us, event | category | flops | bytes accessed | tf_op | source)
XLA Modules:
  0.0 65.2 jit_solution(16263730066902095806)
XLA Ops:
  0.6 22.4 %opponent.1 = (bf16[4,384,256]{2,1,0:T(8,128)(2,1)}, f32[4,24,256]{2,1,0:T(8,128)}, f32[8,8,128]{2,1,0:T(8,128)}) custom-call(bf16[4,32,256]{2,1,0:T(8,128)(2,1)} %upper_ref.1, s32[3,256]{1,0:T(4,128)} %parent_ref.1, s32[1,96]{1,0:T(1,128)} %bitcast.23, s32[5,96]{1,0:T(8,128)} %bitcast.17, f32[1,256]{1,0:T(1,128)} %bitcast.20, ...), custom_call_target="tpu_custom_call" | custom-call | tf_op jit(solution)/shard_map/opponent/pallas_call | solution.py:220
  23.0 37.6 %responder.1 = (f32[4,32,256]{2,1,0:T(8,128)}, f32[1,256]{1,0:T(1,128)}, f32[1,1]{1,0:T(1,128)}) custom-call(bf16[4,384,256]{2,1,0:T(8,128)(2,1)} %get-tuple-element.9.ratio_ref, f32[4,24,256]{2,1,0:T(8,128)} %get-tuple-element.10.reach_ref, f32[8,8,128]{2,1,0:T(8,128)} %get-tuple-element.11.anc_ref, s32[96]{0:T(128)} %actions_ref.1, s32[96,1024]{1,0:T(8,128)} %rank_ref.1, ...), custom_call_target="tpu_custom_call" | custom-call | tf_op jit(solution)/shard_map/responder/pallas_call | solution.py:389
  60.6 1.6 %copy.19 = f32[4,32,256]{2,1,0:T(8,128)} copy(f32[4,32,256]{2,1,0:T(8,128)} %get-tuple-element.18) | data formatting | bytes 262144
  62.2 1.2 %copy.20 = f32[256]{0:T(256)} copy(f32[256]{0:T(256)} %bitcast.21) | data formatting | bytes 2048
